TPU v7x, 32 devices: a whole 2x2x4 slice. The times are simulated.
32 devices in a mesh: expert: 8 (over y, x, core), replica: 4 (over z).
Axes of the slice: x: 2, y: 2, z: 4, core: 2. Of those that a mesh axis runs over, the one named last changes fastest.
Arguments:
- tokens_in: bfloat16 [8192, 2048], P(('expert', 'replica')), may hold values from -6 to 6
- cotangents: bfloat16 [8192, 8192], P(('expert', 'replica')), may hold values from -0.1796875 to 0.1796875
- left_root: bfloat16 [8, 2048, 2048], P('expert'), may hold values from -2 to 6, as said below
- right_root: bfloat16 [8, 8, 1024, 1024], P('expert', 'replica'), may hold values from -2 to 6, as said below
Outputs:
- update: bfloat16 [8, 2048, 8192], P('expert', None, 'replica')
Inputs may be any that keep to these rules, and one draw needn't show every extreme that they name: `left_root`: each matrix is symmetric. `right_root`: each block is symmetric.
All inputs are finite; a program needn't handle non-finite values.
Results may differ from a plain program's by a relative error of at most 0.0058.
Values may be sent and summed in bfloat16 or wider, within the bound.
A program may use at most 192 MiB of HBM per device.

v0:
```python
import jax
import jax.numpy as jnp
from jax import lax
from jax.sharding import PartitionSpec as P


def body(tokens_in, cotangents, left_root, right_root):
    expert_count = lax.axis_size("expert")
    replica_count = lax.axis_size("replica")
    local_experts = left_root.shape[0]
    width = left_root.shape[1]
    block_count = right_root.shape[1]
    block_size = right_root.shape[2]
    columns = cotangents.shape[1] // replica_count
    slot_count = tokens_in.shape[0] // (expert_count * local_experts)
    shaped = cotangents.reshape(1, expert_count, local_experts, slot_count, replica_count, columns)
    routed = lax.all_to_all(
        lax.all_to_all(shaped, "expert", split_axis=1, concat_axis=1, tiled=True),
        "replica",
        split_axis=4,
        concat_axis=0,
        tiled=True,
    )
    routed = routed.reshape(replica_count, expert_count, local_experts, slot_count, columns)
    tokens = tokens_in.reshape(expert_count, local_experts, slot_count, width)
    grouped = lax.all_to_all(tokens, "expert", split_axis=0, concat_axis=0, tiled=True)
    gradient = jnp.einsum(
        "rnxsd,rnxsf->xdf",
        lax.all_gather(grouped[None], "replica", axis=0, tiled=True),
        routed,
        preferred_element_type=jnp.float32,
    )
    gradient = gradient.astype(jnp.bfloat16)
    blocks = gradient.reshape(local_experts, width, block_count, block_size)
    applied = jnp.einsum("xdbk,xbkj->xdbj", blocks, right_root, preferred_element_type=jnp.float32)
    applied = applied.astype(jnp.bfloat16).reshape(local_experts, width, columns)
    update = jnp.einsum("xde,xef->xdf", left_root, applied, preferred_element_type=jnp.float32)
    return update.astype(jnp.bfloat16)


def solution(mesh):
    in_specs = (
        P(("expert", "replica"), None),
        P(("expert", "replica"), None),
        P("expert", None, None),
        P("expert", "replica", None, None),
    )
    out_specs = P("expert", None, "replica")
    return jax.shard_map(body, mesh=mesh, in_specs=in_specs, out_specs=out_specs, check_vma=False)
```

profile of v0, /device:TPU:0, one launch (start us, length us, event | category | flops | bytes accessed | tf_op | source)
XLA Modules:
  0.0 275.7 jit_solution(12691857189009747764)
XLA Ops:
  6.5 5.2 %all-to-all-start = ((bf16[8,1,32,2048]{3,2,1,0:T(8,128)(2,1)}), bf16[8,1,32,2048]{3,2,1,0:T(8,128)(2,1)S(1)}, u32[]{:S(2)}, u32[]{:S(2)}) async-start(bf16[8,1,32,2048]{3,2,1,0:T(8,128)(2,1)} %bitcast.41), calls=%async_computation | async-start | bytes 2097152 | tf_op jit(solution)/shard_map/all_to_all | solution.py:26
  11.7 7.8 %reshape.40 = bf16[1,8,1,32,4,2048]{5,4,3,1,2,0:T(4,128)(2,1)} reshape(bf16[256,8192]{1,0:T(8,128)(2,1)} %param.5) | data formatting | bytes 8388608 | tf_op jit(solution)/shard_map/reshape | solution.py:16
  19.5 6.6 %copy.13 = bf16[1,8,1,32,4,2048]{5,3,4,2,0,1:T(8,128)(2,1)} copy(bf16[1,8,1,32,4,2048]{5,4,3,1,2,0:T(4,128)(2,1)} %reshape.40) | data formatting | bytes 8388608 | tf_op jit(solution)/shard_map/reshape | solution.py:16
  26.1 1.0 all-to-all-done
  27.1 0.0 copy-start
  27.1 4.6 %all-to-all-start.1 = ((bf16[1,8,1,32,4,2048]{5,3,4,2,0,1:T(8,128)(2,1)}), bf16[1,8,1,32,4,2048]{5,3,4,2,0,1:T(8,128)(2,1)}, u32[]{:S(2)}, u32[]{:S(2)}) async-start(bf16[1,8,1,32,4,2048]{5,3,4,2,0,1:T(8,128)(2,1)} %copy.13), calls=%async_computation.1 | async-start | bytes 8388608 | tf_op jit(solution)/shard_map/all_to_all | solution.py:18
  31.7 0.0 all-gather.3.cloned.1.call-start
  31.8 0.0 copy-done
  31.8 0.7 all-gather.3.cloned.1.call-update
  32.4 48.4 %all-to-all-done.1 = bf16[1,8,1,32,4,2048]{5,3,4,2,0,1:T(8,128)(2,1)} async-done(((bf16[1,8,1,32,4,2048]{5,3,4,2,0,1:T(8,128)(2,1)}), bf16[1,8,1,32,4,2048]{5,3,4,2,0,1:T(8,128)(2,1)}, u32[]{:S(2)}, u32[]{:S(2)}) %all-to-all-start.1) | async-done | bytes 4194336 | tf_op jit(solution)/shard_map/all_to_all | solution.py:18
  80.8 4.8 %copy.14 = bf16[1,8,1,32,4,2048]{5,3,1,2,0,4:T(8,128)(2,1)} copy(bf16[1,8,1,32,4,2048]{5,3,4,2,0,1:T(8,128)(2,1)} %all-to-all-done.1) | data formatting | bytes 8388608 | tf_op jit(solution)/shard_map/all_to_all | solution.py:18
  85.6 5.0 %all-to-all-start.2 = ((bf16[1,8,1,32,4,2048]{5,3,1,2,0,4:T(8,128)(2,1)}), bf16[1,8,1,32,4,2048]{5,3,1,2,0,4:T(8,128)(2,1)}, u32[]{:S(2)}, u32[]{:S(2)}) async-start(bf16[1,8,1,32,4,2048]{5,3,1,2,0,4:T(8,128)(2,1)} %copy.14), calls=%async_computation.2 | async-start | bytes 8388608 | tf_op jit(solution)/shard_map/all_to_all | solution.py:17
  90.6 61.0 %all-gather.3.cloned.1.call-done = bf16[32,1,32,2048]{3,2,1,0:T(8,128)(2,1)} async-done(((bf16[8,1,32,2048]{3,2,1,0:T(8,128)(2,1)}), bf16[32,1,32,2048]{3,2,1,0:T(8,128)(2,1)}) %all-gather.3.cloned.1.call-update) | async-done | bytes 4194320 | tf_op jit(solution)/shard_map/all_gather | solution.py:29
  151.6 54.4 %all-to-all-done.2 = bf16[1,8,1,32,4,2048]{5,3,1,2,0,4:T(8,128)(2,1)} async-done(((bf16[1,8,1,32,4,2048]{5,3,1,2,0,4:T(8,128)(2,1)}), bf16[1,8,1,32,4,2048]{5,3,1,2,0,4:T(8,128)(2,1)}, u32[]{:S(2)}, u32[]{:S(2)}) %all-to-all-start.2) | async-done | bytes 4194336 | tf_op jit(solution)/shard_map/all_to_all | solution.py:17
  205.9 0.0 slice-start
  205.9 14.1 %bitcast_convert_fusion = bf16[2048,2048]{0,1:T(8,128)(2,1)} fusion(bf16[1,8,1,32,4,2048]{5,3,1,2,0,4:T(8,128)(2,1)} %all-to-all-done.2, bf16[4,8,32,2048]{3,2,1,0:T(8,128)(2,1)} %bitcast.44), kind=kOutput, calls=%fused_computation | convolution fusion | flops 8594128896 | bytes 16777216 | tf_op jit(solution)/shard_map/rnxsd,rnxsf->xdf/dot_general | solution.py:27
  220.1 0.0 slice-start.1
  220.1 14.8 %convolution_convert_fusion = bf16[2,2048,1024]{1,2,0:T(8,128)(2,1)} fusion(bf16[2048,2,1024]{0,2,1:T(8,128)(2,1)} %bitcast.45, bf16[1,2,1024,1024]{3,2,1,0:T(8,128)(2,1)} %param.7), kind=kOutput, calls=%fused_computation.4 | convolution fusion | flops 8594128896 | bytes 20971520 | tf_op jit(solution)/shard_map/xdbk,xbkj->xdbj/dot_general | solution.py:35
  234.9 0.0 slice-done
  234.9 0.0 slice-done.1
  234.9 21.8 %convert_bitcast_fusion = bf16[1,2048,2048]{1,2,0:T(8,128)(2,1)} fusion(bf16[2048,2048]{0,1:T(8,128)(2,1)} %bitcast.46, bf16[1,2048,2048]{2,1,0:T(8,128)(2,1)S(1)} %bitcast.43), kind=kOutput, calls=%fused_computation.3 | convolution fusion | flops 17184063488 | bytes 25165824 | tf_op jit(solution)/shard_map/xde,xef->xdf/dot_general | solution.py:37
  256.7 12.2 %copy.19 = bf16[1,2048,2048]{2,1,0:T(8,128)(2,1)} copy(bf16[1,2048,2048]{1,2,0:T(8,128)(2,1)} %convert_bitcast_fusion) | data formatting | bytes 16777216 | tf_op jit(solution)/shard_map/convert_element_type | solution.py:38
  (1 shorter events, 0.0 us)
Async XLA Ops:
  6.5 20.6 %all-to-all-start = ((bf16[8,1,32,2048]{3,2,1,0:T(8,128)(2,1)}), bf16[8,1,32,2048]{3,2,1,0:T(8,128)(2,1)S(1)}, u32[]{:S(2)}, u32[]{:S(2)}) async-start(bf16[8,1,32,2048]{3,2,1,0:T(8,128)(2,1)} %bitcast.41), calls=%async_computation | async-start | bytes 2097152 | tf_op jit(solution)/shard_map/all_to_all | solution.py:26
  27.1 4.6 %copy-start = (bf16[8,1,32,2048]{3,2,1,0:T(8,128)(2,1)}, bf16[8,1,32,2048]{3,2,1,0:T(8,128)(2,1)S(1)}, u32[]{:S(2)}) copy-start(bf16[8,1,32,2048]{3,2,1,0:T(8,128)(2,1)S(1)} %all-to-all-done) | copy-start | bytes 3145732
  27.1 53.7 %all-to-all-start.1 = ((bf16[1,8,1,32,4,2048]{5,3,4,2,0,1:T(8,128)(2,1)}), bf16[1,8,1,32,4,2048]{5,3,4,2,0,1:T(8,128)(2,1)}, u32[]{:S(2)}, u32[]{:S(2)}) async-start(bf16[1,8,1,32,4,2048]{5,3,4,2,0,1:T(8,128)(2,1)} %copy.13), calls=%async_computation.1 | async-start | bytes 8388608 | tf_op jit(solution)/shard_map/all_to_all | solution.py:18
  31.7 119.9 %all-gather.3.cloned.1.call-start = ((), (), s32[]{:S(2)}) async-start(), calls=%async_computation.3 | async-start | bytes 5242880 | tf_op jit(solution)/shard_map/all_gather | solution.py:29
  85.6 120.3 %all-to-all-start.2 = ((bf16[1,8,1,32,4,2048]{5,3,1,2,0,4:T(8,128)(2,1)}), bf16[1,8,1,32,4,2048]{5,3,1,2,0,4:T(8,128)(2,1)}, u32[]{:S(2)}, u32[]{:S(2)}) async-start(bf16[1,8,1,32,4,2048]{5,3,1,2,0,4:T(8,128)(2,1)} %copy.14), calls=%async_computation.2 | async-start | bytes 8388608 | tf_op jit(solution)/shard_map/all_to_all | solution.py:17
  205.9 28.9 %slice-start = ((s8[8388608]{0:T(1024)(128)(4,1)}), s8[4194304]{0:T(1024)(128)(4,1)S(1)}, s32[]{:S(2)}) async-start(s8[8388608]{0:T(1024)(128)(4,1)} %bitcast.42), calls=%async_computation.4 | async-start | bytes 8388608
  220.1 14.8 %slice-start.1 = ((s8[8388608]{0:T(1024)(128)(4,1)}), s8[4194304]{0:T(1024)(128)(4,1)S(1)}, s32[]{:S(2)}) async-start(s8[8388608]{0:T(1024)(128)(4,1)} %bitcast.42), calls=%async_computation.5 | async-start | bytes 8388608
Sparse Core Ops, SparseCore 0:
  34.1 117.4 all-gather.2
where the time goes:
time: 277 us; the launch traced here: 276 us
  waiting for transfers between devices  165 us (60%)
  matrix products  50.7 us (18%)
  local copies, waits for them, and re-layouts  31.4 us (11%)
  starting transfers between devices  14.8 us (5%)
  between operations  13.4 us (5%)
    all_gather x1, waiting for transfers between devices, body(): lax.all_gather(grouped[None], 'replica', axis=0, tiled=True)  61 us
    all_to_all x1, waiting for transfers between devices, body(): lax.all_to_all(lax.all_to_all(shaped, 'expert', split_axis=1, concat_axis...  54.4 us
    all_to_all x1, waiting for transfers between devices, body(): lax.all_to_all(shaped, 'expert', split_axis=1, concat_axis=1, tiled=True)  48.4 us
    dot_general x1, matrix products, body(): jnp.einsum('xde,xef->xdf', left_root, applied, preferred_element_type=jnp...  21.8 us
    dot_general x1, matrix products, body(): jnp.einsum('xdbk,xbkj->xdbj', blocks, right_root, preferred_element_type=...  14.8 us
    reshape x2, local copies, waits for them, and re-layouts, body(): cotangents.reshape(1, expert_count, local_experts, slot_count, replica_co...  14.4 us
    dot_general x1, matrix products, body(): jnp.einsum('rnxsd,rnxsf->xdf', lax.all_gather(grouped[None], 'replica', a...  14.1 us
    convert_element_type x1, local copies, waits for them, and re-layouts, body(): return update.astype(jnp.bfloat16)  12.2 us
  transfers between devices with their start and end apart: 4, of which 4 were waited for; matrix products, arithmetic and copies ran while one was open for 7% of the time, Pallas kernels for 0%

commit v1 on v0

--- a/solution.py
+++ b/solution.py
@@ -2,6 +2,18 @@
 import jax.numpy as jnp
 from jax import lax
 from jax.sharding import PartitionSpec as P
+
+
+def product_in_turn(x, axis, dim, term):
+    size, index, extent = (lax.axis_size(axis), lax.axis_index(axis), x.shape[dim])
+    right = [(i, (i + 1) % size) for i in range(size)]
+    carried, total = (x, None)
+    for hop in range(size):
+        arriving = lax.ppermute(carried, axis, right) if hop < size - 1 else None
+        take_in = term(carried, (index - hop) % size * extent)
+        total = take_in if total is None else total + take_in
+        carried = arriving
+    return total
 
 
 def body(tokens_in, cotangents, left_root, right_root):
@@ -24,11 +36,16 @@
     routed = routed.reshape(replica_count, expert_count, local_experts, slot_count, columns)
     tokens = tokens_in.reshape(expert_count, local_experts, slot_count, width)
     grouped = lax.all_to_all(tokens, "expert", split_axis=0, concat_axis=0, tiled=True)
-    gradient = jnp.einsum(
-        "rnxsd,rnxsf->xdf",
-        lax.all_gather(grouped[None], "replica", axis=0, tiled=True),
-        routed,
-        preferred_element_type=jnp.float32,
+    gradient = product_in_turn(
+        grouped[None],
+        "replica",
+        0,
+        lambda own_block, start: jnp.einsum(
+            "rnxsd,rnxsf->xdf",
+            own_block,
+            lax.dynamic_slice_in_dim(routed, start, own_block.shape[0], axis=0),
+            preferred_element_type=jnp.float32,
+        ),
     )
     gradient = gradient.astype(jnp.bfloat16)
     blocks = gradient.reshape(local_experts, width, block_count, block_size)

time: 277 us -> 347 us (1.25)
  blocking collectives: 0 us -> 54.1 us
  matrix products: 50.7 us -> 85.4 us
  waiting for transfers between devices: 165 us -> 140 us
  starting transfers between devices: 14.8 us -> 36.8 us
  between operations: 13.4 us -> 0.03 us
    ppermute x0 -> x3, waiting for transfers between devices: none -> 108 us  [product_in_turn(): arriving = lax.ppermute(carried, axis, right) if hop < size - 1 else None]
    all_gather x1 -> x0, waiting for transfers between devices: 61 us -> none  [body(): lax.all_gather(grouped[None], 'replica', axis=0, tiled=True)]
    all_to_all x0 -> x1, blocking collectives: none -> 54.1 us  [body(): lax.all_to_all(shaped, 'expert', split_axis=1, concat_axis=1, tiled=True)]
    all_to_all x1 -> x0, waiting for transfers between devices: 48.4 us -> none  [body(): lax.all_to_all(shaped, 'expert', split_axis=1, concat_axis=1, tiled=True)]
    dot_general x1 -> x4, matrix products: 14.1 us -> 49.2 us  [body(): jnp.einsum('rnxsd,rnxsf->xdf', own_block, lax.dynamic_slice_in_dim(routed...]
    all_to_all x1, waiting for transfers between devices: 54.4 us -> 21.8 us  [body(): lax.all_to_all(lax.all_to_all(shaped, 'expert', split_axis=1, concat_axis...]
    ppermute x0 -> x3, starting transfers between devices: none -> 28.4 us  [product_in_turn(): arriving = lax.ppermute(carried, axis, right) if hop < size - 1 else None]
    all_to_all x1, waiting for transfers between devices: 1 us -> 10.5 us  [body(): lax.all_to_all(tokens, 'expert', split_axis=0, concat_axis=0, tiled=True)]
  transfers between devices with their start and end apart: 4 -> 5, of which waited for: 4 -> 4; matrix products, arithmetic and copies ran while one was open for 7% -> 10% of each run, Pallas kernels for 0% -> 0%
where the time goes in v1:
time: 347 us; the launch traced here: 346 us
  waiting for transfers between devices  140 us (40%)
  matrix products  85.4 us (25%)
  blocking collectives  54.1 us (16%)
  starting transfers between devices  36.8 us (11%)
  local copies, waits for them, and re-layouts  29.4 us (8%)
    ppermute x3, waiting for transfers between devices, product_in_turn(): arriving = lax.ppermute(carried, axis, right) if hop < size - 1 else None  108 us
    all_to_all x1, blocking collectives, body(): lax.all_to_all(shaped, 'expert', split_axis=1, concat_axis=1, tiled=True)  54.1 us
    dot_general x4, matrix products, body(): jnp.einsum('rnxsd,rnxsf->xdf', own_block, lax.dynamic_slice_in_dim(routed...  49.2 us
    ppermute x3, starting transfers between devices, product_in_turn(): arriving = lax.ppermute(carried, axis, right) if hop < size - 1 else None  28.4 us
    all_to_all x1, waiting for transfers between devices, body(): lax.all_to_all(lax.all_to_all(shaped, 'expert', split_axis=1, concat_axis...  21.8 us
    dot_general x1, matrix products, body(): jnp.einsum('xde,xef->xdf', left_root, applied, preferred_element_type=jnp...  21.6 us
    dot_general x1, matrix products, body(): jnp.einsum('xdbk,xbkj->xdbj', blocks, right_root, preferred_element_type=...  14.6 us
    reshape x2, local copies, waits for them, and re-layouts, body(): cotangents.reshape(1, expert_count, local_experts, slot_count, replica_co...  12.4 us
  transfers between devices with their start and end apart: 5, of which 4 were waited for; matrix products, arithmetic and copies ran while one was open for 10% of the time, Pallas kernels for 0%

profile of v1, /device:TPU:0, one launch (start us, length us, event | category | flops | bytes accessed | tf_op | source)
XLA Modules:
  0.0 346.0 jit_solution(11676960317589416908)
XLA Ops:
  0.0 7.8 %reshape.86 = bf16[1,8,1,32,4,2048]{5,4,3,1,2,0:T(4,128)(2,1)} reshape(bf16[256,8192]{1,0:T(8,128)(2,1)} %param.5) | data formatting | bytes 8388608 | tf_op jit(solution)/shard_map/reshape | solution.py:28
  7.8 4.6 %copy.13 = bf16[1,8,1,32,4,2048]{5,3,4,2,0,1:T(8,128)(2,1)S(1)} copy(bf16[1,8,1,32,4,2048]{5,4,3,1,2,0:T(4,128)(2,1)} %reshape.86) | data formatting | bytes 8388608 | tf_op jit(solution)/shard_map/reshape | solution.py:28
  12.4 54.1 %all_to_all.19 = bf16[1,8,1,32,4,2048]{5,3,4,2,0,1:T(8,128)(2,1)} all-to-all(bf16[1,8,1,32,4,2048]{5,3,4,2,0,1:T(8,128)(2,1)S(1)} %copy.13), channel_id=1, replica_groups=mesh['expert'=8,'replica'=4] {'expert'}, dimensions={1} | all-to-all | bytes 8388608 | tf_op jit(solution)/shard_map/all_to_all | solution.py:30
  66.5 3.6 %all-to-all-start.2 = ((bf16[8,1,32,2048]{3,2,1,0:T(8,128)(2,1)}), bf16[8,1,32,2048]{3,2,1,0:T(8,128)(2,1)S(1)}, u32[]{:S(2)}, u32[]{:S(2)}) async-start(bf16[8,1,32,2048]{3,2,1,0:T(8,128)(2,1)} %bitcast.1), calls=%async_computation.2 | async-start | bytes 2097152 | tf_op jit(solution)/shard_map/all_to_all | solution.py:38
  70.1 4.8 %copy.14 = bf16[1,8,1,32,4,2048]{5,3,1,2,0,4:T(8,128)(2,1)} copy(bf16[1,8,1,32,4,2048]{5,3,4,2,0,1:T(8,128)(2,1)} %all_to_all.19) | data formatting | bytes 8388608 | tf_op jit(solution)/shard_map/all_to_all | solution.py:30
  74.9 10.5 %all-to-all-done.2 = bf16[8,1,32,2048]{3,2,1,0:T(8,128)(2,1)S(1)} async-done(((bf16[8,1,32,2048]{3,2,1,0:T(8,128)(2,1)}), bf16[8,1,32,2048]{3,2,1,0:T(8,128)(2,1)S(1)}, u32[]{:S(2)}, u32[]{:S(2)}) %all-to-all-start.2) | async-done | bytes 1048608 | tf_op jit(solution)/shard_map/all_to_all | solution.py:38
  85.4 4.9 %all-to-all-start.1 = ((bf16[1,8,1,32,4,2048]{5,3,1,2,0,4:T(8,128)(2,1)}), bf16[1,8,1,32,4,2048]{5,3,1,2,0,4:T(8,128)(2,1)}, u32[]{:S(2)}, u32[]{:S(2)}) async-start(bf16[1,8,1,32,4,2048]{5,3,1,2,0,4:T(8,128)(2,1)} %copy.14), calls=%async_computation.1 | async-start | bytes 8388608 | tf_op jit(solution)/shard_map/all_to_all | solution.py:29
  90.3 2.0 collective-permute-start
  92.3 89.7 %collective-permute-done = bf16[1,8,1,32,2048]{4,3,1,2,0:T(8,128)(2,1)S(1)} collective-permute-done((bf16[1,8,1,32,2048]{4,3,1,2,0:T(8,128)(2,1)S(1)}, bf16[1,8,1,32,2048]{4,3,1,2,0:T(8,128)(2,1)S(1)}, u32[]{:S(2)}, u32[]{:S(2)}) %collective-permute-start) | collective-permute-done | bytes 1048608 | tf_op jit(solution)/shard_map/ppermute | solution.py:12
  182.0 21.3 %collective-permute-start.1 = (bf16[1,8,1,32,2048]{4,3,1,2,0:T(8,128)(2,1)S(1)}, bf16[1,8,1,32,2048]{4,3,1,2,0:T(8,128)(2,1)S(1)}, u32[]{:S(2)}, u32[]{:S(2)}) collective-permute-start(bf16[1,8,1,32,2048]{4,3,1,2,0:T(8,128)(2,1)S(1)} %collective-permute-done), channel_id=1, source_target_pairs={{0,1},{1,2},{2,3},{3,0},{4,5},{5,6},{6,7},{7,4},{8,9},{9,10},{10,1... | collective-permute-start | bytes 3145736 | tf_op jit(solution)/shard_map/ppermute | solution.py:12
  203.3 18.2 %collective-permute-done.1 = bf16[1,8,1,32,2048]{4,3,1,2,0:T(8,128)(2,1)S(1)} collective-permute-done((bf16[1,8,1,32,2048]{4,3,1,2,0:T(8,128)(2,1)S(1)}, bf16[1,8,1,32,2048]{4,3,1,2,0:T(8,128)(2,1)S(1)}, u32[]{:S(2)}, u32[]{:S(2)}) %collective-permute-start.1) | collective-permute-done | bytes 1048608 | tf_op jit(solution)/shard_map/ppermute | solution.py:12
  221.5 5.1 %collective-permute-start.2 = (bf16[1,8,1,32,2048]{4,3,1,2,0:T(8,128)(2,1)S(1)}, bf16[1,8,1,32,2048]{4,3,1,2,0:T(8,128)(2,1)}, u32[]{:S(2)}, u32[]{:S(2)}) collective-permute-start(bf16[1,8,1,32,2048]{4,3,1,2,0:T(8,128)(2,1)S(1)} %collective-permute-done.1), channel_id=1, source_target_pairs={{0,1},{1,2},{2,3},{3,0},{4,5},{5,6},{6,7},{7,4},{8,9},{9,10},{10,1... | collective-permute-start | bytes 3145736 | tf_op jit(solution)/shard_map/ppermute | solution.py:12
  226.6 21.8 %all-to-all-done.1 = bf16[1,8,1,32,4,2048]{5,3,1,2,0,4:T(8,128)(2,1)} async-done(((bf16[1,8,1,32,4,2048]{5,3,1,2,0,4:T(8,128)(2,1)}), bf16[1,8,1,32,4,2048]{5,3,1,2,0,4:T(8,128)(2,1)}, u32[]{:S(2)}, u32[]{:S(2)}) %all-to-all-start.1) | async-done | bytes 4194336 | tf_op jit(solution)/shard_map/all_to_all | solution.py:29
  248.3 9.3 %fusion.8 = f32[2048,2048,1]{1,0,2:T(8,128)} fusion(bf16[1,8,1,32,2048]{4,3,1,2,0:T(8,128)(2,1)S(1)} %collective-permute-done.1, bf16[1,8,1,32,4,2048]{5,3,1,2,0,4:T(8,128)(2,1)} %all-to-all-done.1, s32[]{:T(128)S(6)} %select_n.36), kind=kOutput, calls=%fused_computation.11 | convolution fusion | flops 2147483648 | bytes 18874372 | tf_op jit(solution)/shard_map/rnxsd,rnxsf->xdf/dot_general | solution.py:43
  257.7 9.3 %fusion.11 = f32[2048,2048,1]{1,0,2:T(8,128)} fusion(bf16[1,8,1,32,2048]{4,3,1,2,0:T(8,128)(2,1)S(1)} %collective-permute-done, bf16[1,8,1,32,4,2048]{5,3,1,2,0,4:T(8,128)(2,1)} %all-to-all-done.1, s32[]{:T(128)S(6)} %select_n.34), kind=kOutput, calls=%fused_computation.14 | convolution fusion | flops 2147483648 | bytes 18874372 | tf_op jit(solution)/shard_map/rnxsd,rnxsf->xdf/dot_general | solution.py:43
  267.0 0.0 slice-start
  267.0 9.5 %fusion.14 = f32[2048,2048,1]{1,0,2:T(8,128)} fusion(bf16[8,1,32,2048]{3,2,1,0:T(8,128)(2,1)S(1)} %all-to-all-done.2, bf16[1,8,1,32,4,2048]{5,3,1,2,0,4:T(8,128)(2,1)} %all-to-all-done.1, s32[]{:T(128)S(6)} %select_n.32), kind=kOutput, calls=%fused_computation.17 | convolution fusion | flops 2147483648 | bytes 18874372 | tf_op jit(solution)/shard_map/rnxsd,rnxsf->xdf/dot_general | solution.py:43
  276.5 0.0 slice-start.1
  276.5 0.0 collective-permute-done.2
  276.5 21.1 %fusion = bf16[2048,2048]{1,0:T(8,128)(2,1)} fusion(f32[2048,2048,1]{1,0,2:T(8,128)} %fusion.8, f32[2048,2048,1]{1,0,2:T(8,128)} %fusion.11, f32[2048,2048,1]{1,0,2:T(8,128)} %fusion.14, bf16[1,8,1,32,2048]{4,3,1,2,0:T(8,128)(2,1)} %collective-permute-done.2, bf16[1,8,1,32,4,2048]{5,3,1,2,0,4:T(8,128)(2,1)} %all-to-all-done.1, s32[]{:T(128)S(6)} %select_n.38), kind=kOutput, calls=%fused_computation.1 | convolution fusion | flops 2164260864 | bytes 60817412 | tf_op jit(solution)/shard_map/rnxsd,rnxsf->xdf/dot_general | solution.py:43
  297.6 14.6 %convolution_convert_fusion = bf16[2,2048,1024]{1,2,0:T(8,128)(2,1)} fusion(bf16[2048,2,1024]{0,2,1:T(8,128)(2,1)} %bitcast.67, bf16[1,2,1024,1024]{3,2,1,0:T(8,128)(2,1)} %param.7), kind=kOutput, calls=%fused_computation.7 | convolution fusion | flops 8594128896 | bytes 20971520 | tf_op jit(solution)/shard_map/xdbk,xbkj->xdbj/dot_general | solution.py:52
  312.2 0.0 slice-done
  312.2 0.0 slice-done.1
  312.2 21.6 %convert_bitcast_fusion = bf16[1,2048,2048]{1,2,0:T(8,128)(2,1)} fusion(bf16[2048,2048]{0,1:T(8,128)(2,1)} %bitcast.68, bf16[1,2048,2048]{2,1,0:T(8,128)(2,1)S(1)} %bitcast.66), kind=kOutput, calls=%fused_computation.6 | convolution fusion | flops 17184063488 | bytes 25165824 | tf_op jit(solution)/shard_map/xde,xef->xdf/dot_general | solution.py:54
  333.7 12.2 %copy.17 = bf16[1,2048,2048]{2,1,0:T(8,128)(2,1)} copy(bf16[1,2048,2048]{1,2,0:T(8,128)(2,1)} %convert_bitcast_fusion) | data formatting | bytes 16777216 | tf_op jit(solution)/shard_map/convert_element_type | solution.py:55
  (1 shorter events, 0.0 us)
Async XLA Ops:
  66.5 18.9 %all-to-all-start.2 = ((bf16[8,1,32,2048]{3,2,1,0:T(8,128)(2,1)}), bf16[8,1,32,2048]{3,2,1,0:T(8,128)(2,1)S(1)}, u32[]{:S(2)}, u32[]{:S(2)}) async-start(bf16[8,1,32,2048]{3,2,1,0:T(8,128)(2,1)} %bitcast.1), calls=%async_computation.2 | async-start | bytes 2097152 | tf_op jit(solution)/shard_map/all_to_all | solution.py:38
  85.4 162.9 %all-to-all-start.1 = ((bf16[1,8,1,32,4,2048]{5,3,1,2,0,4:T(8,128)(2,1)}), bf16[1,8,1,32,4,2048]{5,3,1,2,0,4:T(8,128)(2,1)}, u32[]{:S(2)}, u32[]{:S(2)}) async-start(bf16[1,8,1,32,4,2048]{5,3,1,2,0,4:T(8,128)(2,1)} %copy.14), calls=%async_computation.1 | async-start | bytes 8388608 | tf_op jit(solution)/shard_map/all_to_all | solution.py:29
  90.3 91.7 %collective-permute-start = (bf16[1,8,1,32,2048]{4,3,1,2,0:T(8,128)(2,1)S(1)}, bf16[1,8,1,32,2048]{4,3,1,2,0:T(8,128)(2,1)S(1)}, u32[]{:S(2)}, u32[]{:S(2)}) collective-permute-start(bf16[1,8,1,32,2048]{4,3,1,2,0:T(8,128)(2,1)S(1)} %bitcast.64), channel_id=1, source_target_pairs={{0,1},{1,2},{2,3},{3,0},{4,5},{5,6},{6,7},{7,4},{8,9},{9,10},{10,1... | collective-permute-start | bytes 3145736 | tf_op jit(solution)/shard_map/ppermute | solution.py:12
  182.0 39.5 %collective-permute-start.1 = (bf16[1,8,1,32,2048]{4,3,1,2,0:T(8,128)(2,1)S(1)}, bf16[1,8,1,32,2048]{4,3,1,2,0:T(8,128)(2,1)S(1)}, u32[]{:S(2)}, u32[]{:S(2)}) collective-permute-start(bf16[1,8,1,32,2048]{4,3,1,2,0:T(8,128)(2,1)S(1)} %collective-permute-done), channel_id=1, source_target_pairs={{0,1},{1,2},{2,3},{3,0},{4,5},{5,6},{6,7},{7,4},{8,9},{9,10},{10,1... | collective-permute-start | bytes 3145736 | tf_op jit(solution)/shard_map/ppermute | solution.py:12
  221.5 55.0 %collective-permute-start.2 = (bf16[1,8,1,32,2048]{4,3,1,2,0:T(8,128)(2,1)S(1)}, bf16[1,8,1,32,2048]{4,3,1,2,0:T(8,128)(2,1)}, u32[]{:S(2)}, u32[]{:S(2)}) collective-permute-start(bf16[1,8,1,32,2048]{4,3,1,2,0:T(8,128)(2,1)S(1)} %collective-permute-done.1), channel_id=1, source_target_pairs={{0,1},{1,2},{2,3},{3,0},{4,5},{5,6},{6,7},{7,4},{8,9},{9,10},{10,1... | collective-permute-start | bytes 3145736 | tf_op jit(solution)/shard_map/ppermute | solution.py:12
  267.0 45.2 %slice-start = ((s8[8388608]{0:T(1024)(128)(4,1)}), s8[4194304]{0:T(1024)(128)(4,1)S(1)}, s32[]{:S(2)}) async-start(s8[8388608]{0:T(1024)(128)(4,1)} %bitcast.65), calls=%async_computation.3 | async-start | bytes 8388608
  276.5 35.7 %slice-start.1 = ((s8[8388608]{0:T(1024)(128)(4,1)}), s8[4194304]{0:T(1024)(128)(4,1)S(1)}, s32[]{:S(2)}) async-start(s8[8388608]{0:T(1024)(128)(4,1)} %bitcast.65), calls=%async_computation.4 | async-start | bytes 8388608
